TPU v7x, 32 devices: a whole 2x2x4 slice. The times are simulated.
32 devices in a mesh: crop: 1, dap: 32 (over z, y, x, core).
Axes of the slice: x: 2, y: 2, z: 4, core: 2. Of those that a mesh axis runs over, the one named last changes fastest.
Arguments:
- homolog_features: bfloat16 [128, 128, 256], P(('crop', 'dap')), may hold values from -6 to 6
- twofold_features: bfloat16 [128, 128, 128], P(('crop', 'dap')), may hold values from -6 to 6
- twofold_offset_map: bfloat16 [128, 8], replicated, may hold values from -0.5 to 0.5
- horizontal_attend_entry_maps: bfloat16 [256, 1024], replicated, may hold values from -2 to 2
- horizontal_attend_exit_map: bfloat16 [256, 256], replicated, may hold values from -0.375 to 0.375
- vertical_attend_entry_maps: bfloat16 [256, 1024], replicated, may hold values from -2 to 2
- vertical_attend_exit_map: bfloat16 [256, 256], replicated, may hold values from -0.375 to 0.375
- tensor_product_factors: bfloat16 [256, 64], replicated, may hold values from -0.375 to 0.375
- tensor_product_exit_map: bfloat16 [1024, 128], replicated, may hold values from -1 to 1
Outputs:
- alignment_output: bfloat16 [128, 128, 256], P('crop', 'dap')
- pair_output: bfloat16 [128, 128, 128], P(('crop', 'dap'))
All inputs are finite; a program needn't handle non-finite values.
Results may differ from a plain program's by a relative error of at most 0.0085.
Values may be sent and summed in bfloat16 or wider, within the bound.
No kernel may reach another device: no remote copies, remote signals or barrier semaphores. Data moves between devices by JAX's collectives and lax.ppermute only.
A program may use at most 64 MiB of HBM per device.

v0:
```python
import functools
import math

import jax
import jax.numpy as jnp
from jax import lax
from jax.experimental import pallas as pl
from jax.experimental.pallas import tpu as pltpu
from jax.sharding import PartitionSpec as P


EPSILON = 1e-05
LANES = 128
F32 = jnp.float32
BF16 = jnp.bfloat16
VMEM = pl.BlockSpec(memory_space=pltpu.VMEM)
SMEM = pl.BlockSpec(memory_space=pltpu.SMEM)


def standardize(values):
    center = values - jnp.mean(values, axis=-1, keepdims=True)
    spread = jnp.mean(center * center, axis=-1, keepdims=True)
    return (center * lax.rsqrt(spread + EPSILON)).astype(BF16)


def dot(left, right):
    return jnp.dot(left, right, preferred_element_type=F32)


def dot_t(left, right):
    return lax.dot_general(left, right, (((1,), (1,)), ((), ())), preferred_element_type=F32)


def call(body, out_shapes, args, scratch=(), limit=16 << 20, flops=0, far=()):
    scalars = [jnp.issubdtype(arg.dtype, jnp.integer) for arg in args]
    return pl.pallas_call(
        body,
        out_shape=[
            pltpu.VMEM(shape, dtype) if near else jax.ShapeDtypeStruct(shape, dtype)
            for shape, dtype, near in out_shapes
        ],
        in_specs=[SMEM if scalar else VMEM for scalar in scalars],
        out_specs=[VMEM] * len(out_shapes),
        scratch_shapes=list(scratch),
        cost_estimate=pl.CostEstimate(flops=flops, bytes_accessed=0, transcendentals=0),
        compiler_params=pltpu.CompilerParams(vmem_limit_bytes=limit),
    )(*[
        arg
        if scalar
        else pltpu.with_memory_space_constraint(arg, pltpu.HBM if at in far else pltpu.VMEM)
        for at, (arg, scalar) in enumerate(zip(args, scalars))
    ])


def lane_masks(width, rows):
    lane = lax.broadcasted_iota(jnp.int32, (rows, LANES), 1)
    return [
        (lane >= start) & (lane < start + width) for start in range(0, LANES, width)
    ]


def masked_rows(block, masks):
    zero = jnp.zeros_like(block)
    return jnp.concatenate([jnp.where(mask, block, zero) for mask in masks], axis=0)


def bias_body(pair_ref, map_ref, out_ref, *, copies):
    rows, _, _ = pair_ref.shape
    heads = map_ref.shape[0]
    height = heads * rows
    row = lax.broadcasted_iota(jnp.int32, (height, heads), 0)
    head = lax.broadcasted_iota(jnp.int32, (height, heads), 1)
    total = None
    for at in range(rows):
        spread = jnp.where(row == head * rows + at, 1.0, 0.0).astype(BF16)
        weights = dot(spread, map_ref[...]).astype(BF16)
        part = dot_t(weights, standardize(pair_ref[at].astype(F32)))
        total = part if total is None else total + part
    block = total.astype(BF16)
    half = height // 2
    for copy in range(copies):
        out_ref[copy * half : (copy + 1) * half, :] = block[copy % 2 * half : (copy % 2 + 1) * half, :]


def scores_of(proj, head_size, masks):
    width = proj.shape[1] // 4
    scale = 1.0 / math.sqrt(head_size)
    scores = []
    for start in range(0, width, LANES):
        queries = proj[:, start : start + LANES]
        keys = masked_rows(proj[:, width + start : width + start + LANES], masks)
        scores.append(dot_t(queries, keys) * scale)
    return scores


def attended_of(scores, values, gates, masks):
    keys = values.shape[0]
    pieces = []
    for at in range(len(masks)):
        piece = scores[at]
        highest = jnp.max(piece, axis=-1, keepdims=True)
        pieces.append(jnp.exp(piece - highest).astype(BF16))
    ones = jnp.ones((keys, LANES), BF16)
    table = jnp.concatenate([masked_rows(values, masks), masked_rows(ones, masks)], axis=1)
    sums = dot(jnp.concatenate(pieces, axis=1), table)
    gate = jax.nn.sigmoid(gates.astype(F32))
    return (gate * (sums[:, :LANES] / sums[:, LANES:])).astype(BF16)


def row_scores_body(features_ref, maps_ref, kept_ref, scores_ref, *, head_size):
    sequences, residues, channels = features_ref.shape
    features = features_ref[...].reshape(sequences * residues, channels)
    proj = dot(standardize(features.astype(F32)), maps_ref[...]).astype(BF16)
    for block, start in enumerate(range(0, channels, LANES)):
        kept_ref[block, :, :LANES] = proj[:, 2 * channels + start : 2 * channels + start + LANES]
        kept_ref[block, :, LANES : 2 * LANES] = proj[:, 3 * channels + start : 3 * channels + start + LANES]
        kept_ref[block, :, 2 * LANES :] = features[:, start : start + LANES]
    masks = lane_masks(head_size, residues)
    for at in range(sequences):
        mine = proj[at * residues : (at + 1) * residues, :]
        for block, scores in enumerate(scores_of(mine, head_size, masks)):
            scores_ref[at, block] = scores


def row_half(bias_ref, kept_ref, scores_ref, wide, bias, first, blocks, head_size):
    sequences, _, residues, _ = scores_ref.shape
    rows = residues // blocks
    heads = bias_ref.shape[0] // residues
    masks = lane_masks(head_size, residues)
    wide[...] = bias_ref[...].astype(F32)
    for source in range(blocks):
        for head in range(heads):
            start = (source * heads + head) * rows
            bias[head, source * rows : (source + 1) * rows, :] = wide[start : start + rows, :]
    gated = []
    for block in range(heads // len(masks)):
        parts = []
        for at in range(sequences):
            mine = pl.ds(at * residues, residues)
            scores = [
                scores_ref[at, first + block, :, k * residues : (k + 1) * residues]
                + bias[block * len(masks) + k]
                for k in range(len(masks))
            ]
            values = kept_ref[first + block, mine, :LANES]
            gates = kept_ref[first + block, mine, LANES : 2 * LANES]
            parts.append(attended_of(scores, values, gates, masks))
        gated.append(parts)
    return gated


def row_first_body(me_ref, bias_ref, kept_ref, scores_ref, out_ref, wide, bias, *, blocks, head_size):
    groups = kept_ref.shape[0] // 2
    residues = scores_ref.shape[2]
    first = jnp.bitwise_and(me_ref[0], 1) * groups
    gated = row_half(bias_ref, kept_ref, scores_ref, wide, bias, first, blocks, head_size)
    for block, parts in enumerate(gated):
        for at, part in enumerate(parts):
            out_ref[block, at * residues : (at + 1) * residues, :] = part


def row_second_body(
    me_ref, bias_ref, kept_ref, scores_ref, gated_ref, exit_ref, out_ref, wide, bias, sent, *, blocks, head_size
):
    groups = kept_ref.shape[0] // 2
    sequences, tiles, residues, _ = scores_ref.shape
    rows = residues // blocks
    parity = jnp.bitwise_and(me_ref[0], 1)
    gated = row_half(bias_ref, kept_ref, scores_ref, wide, bias, (1 - parity) * groups, blocks, head_size)

    def exit_rows(group):
        return exit_ref[pl.ds(pl.multiple_of(group * LANES, LANES), LANES), :]

    for at in range(sequences):
        mine = slice(at * residues, (at + 1) * residues)
        delta = None
        for block in range(groups):
            for part, group in (
                (gated_ref[block, mine, :], parity * groups + block),
                (gated[block][at], (1 - parity) * groups + block),
            ):
                more = dot(part, exit_rows(group))
                delta = more if delta is None else delta + more
        for tile in range(tiles):
            line = kept_ref[tile, mine, 2 * LANES :].astype(F32) + delta[:, tile * LANES : (tile + 1) * LANES]
            for target in range(blocks):
                start = ((target * sequences + at) * tiles + tile) * rows
                sent[start : start + rows, :] = line[target * rows : (target + 1) * rows, :]
    out_ref[...] = sent[...].astype(BF16)


def column_body(
    received_ref, maps_ref, exit_ref, factors_ref, lines_ref, left_ref, right_ref, wide, proj_ref, score_ref, turned,
    *, rows, head_size
):
    channels = maps_ref.shape[0]
    tiles = channels // LANES
    sequences = received_ref.shape[0] // (rows * tiles)
    span = factors_ref.shape[0] // 2
    wide[...] = received_ref[...].astype(F32)
    if left_ref.shape[0] > rows * span:
        left_ref[...] = jnp.zeros_like(left_ref)
    masks = lane_masks(head_size, sequences)
    chosen = [
        [pl.ds(tile * rows + at, sequences, stride=tiles * rows) for tile in range(tiles)]
        for at in range(rows)
    ]
    lines = jnp.concatenate(
        [jnp.concatenate([wide[rows_of, :] for rows_of in one], axis=1) for one in chosen], axis=0
    )
    proj_ref[...] = dot(standardize(lines), maps_ref[...]).astype(BF16)
    for at in range(rows):
        proj = proj_ref[at * sequences : (at + 1) * sequences, :]
        for block, scores in enumerate(scores_of(proj, head_size, masks)):
            score_ref[at, block] = scores
    gated = []
    for at in range(rows):
        mine = slice(at * sequences, (at + 1) * sequences)
        parts = []
        for block, start in enumerate(range(0, channels, LANES)):
            scores = [
                score_ref[at, block, :, k * sequences : (k + 1) * sequences] for k in range(len(masks))
            ]
            values = proj_ref[mine, 2 * channels + start : 2 * channels + start + LANES]
            gates = proj_ref[mine, 3 * channels + start : 3 * channels + start + LANES]
            parts.append(attended_of(scores, values, gates, masks))
        gated.append(jnp.concatenate(parts, axis=1))
    lines = lines + dot(jnp.concatenate(gated, axis=0), exit_ref[...])
    lines = lines.astype(BF16).astype(F32)
    lines_ref[...] = lines
    factors = dot_t(factors_ref[...], standardize(lines))
    for at in range(rows):
        mine = slice(at * sequences, (at + 1) * sequences)
        left_ref[at * span : (at + 1) * span, :] = factors[:span, mine].astype(BF16)
        turned[pl.ds(at, span, stride=rows), :] = factors[span:, mine]
    right_ref[...] = turned[...].astype(BF16)


def arrange_body(lines_ref, out_ref, done, *, rows):
    total, channels = lines_ref.shape
    sequences = total // rows
    tiles = channels // LANES
    for at in range(rows):
        for tile in range(tiles):
            done[pl.ds(tile * rows + at, sequences, stride=tiles * rows), :] = lines_ref[
                at * sequences : (at + 1) * sequences, tile * LANES : (tile + 1) * LANES
            ]
    out_ref[...] = done[...].astype(BF16)


def table_body(exit_ref, out_ref, wide):
    depth = exit_ref.shape[1]
    span = math.isqrt(exit_ref.shape[0])
    wide[...] = exit_ref[...].astype(F32)
    zero = jnp.zeros((span, depth), BF16)
    for e in range(span):
        weights = wide[pl.ds(e, span, stride=span), :].astype(BF16)
        for row, side in enumerate(([weights, zero], [zero, weights])):
            start = (2 * e + row) * span
            out_ref[start : start + span, :] = jnp.concatenate(side, axis=1)


def outer_rows(left_ref, right_refs, out_ref, product, order, span, count, rows):
    width = rows * span
    lanes = left_ref.shape[0]
    residues = len(order) * rows
    left = left_ref[...]
    zero = jnp.zeros_like(left)
    both = jnp.concatenate(
        [jnp.concatenate([left, zero], axis=1), jnp.concatenate([zero, left], axis=1)], axis=0
    )
    half = len(order) // 2
    lane = lax.broadcasted_iota(jnp.int32, (residues, LANES), 1)
    for piece, right_ref in enumerate(right_refs):
        products = dot_t(
            jnp.concatenate([right_ref[: half * width, :], right_ref[half * width :, :]], axis=1), both
        ) * (1.0 / count)
        for at in range(len(order)):
            start = at % half * width
            side = at // half * lanes
            for tile in range(lanes // LANES):
                product[tile, at] = products[
                    start : start + width, side + tile * LANES : side + (tile + 1) * LANES
                ]
        for e in range(0, span, 2):
            for tile in range(lanes // LANES):
                halves = couple_of(product, tile, e, rows, residues)
                swapped = [pltpu.roll(part, LANES // 2, 1) for part in halves]
                for pair in range(2 * tile, min(2 * tile + 2, rows // 2)):
                    low, high = (halves[0], swapped[1]) if pair % 2 == 0 else (swapped[0], halves[1])
                    start = (piece * (rows // 2) + pair) * residues
                    out_ref[start : start + residues, e // 2 * LANES : (e // 2 + 1) * LANES] = jnp.where(
                        lane < LANES // 2, low, high
                    ).astype(BF16)


def couple_of(product, tile, e, rows, residues):
    if rows % 8 == 0:
        return [
            product[tile, :, (e + odd) * rows : (e + odd + 1) * rows, :].reshape(residues, LANES)
            for odd in (0, 1)
        ]
    couples = product[tile, :, e * rows : (e + 2) * rows, :]
    sources = couples.shape[0]
    if rows != 4:
        return [
            jnp.concatenate([couples[at, odd * rows : (odd + 1) * rows] for at in range(sources)], axis=0)
            for odd in (0, 1)
        ]
    couples = couples.reshape(sources // 2, 2, 2 * rows, LANES)
    first, second = couples[:, 0], couples[:, 1]
    upper = lax.broadcasted_iota(jnp.int32, first.shape, 1) < rows
    even = jnp.where(upper, first, pltpu.roll(second, rows, 1))
    odd = jnp.where(upper, pltpu.roll(first, rows, 1), second)
    return [part.reshape(residues, LANES) for part in (even, odd)]


def outer_first_body(left_ref, right_ref, out_ref, product, **sizes):
    outer_rows(left_ref, [right_ref], out_ref, product, **sizes)


def outer_last_body(me_ref, left_ref, *refs, radix, order, rows, **sizes):
    right_refs = refs[: radix - 1]
    table_ref, first_ref, pair_ref, out_ref, product, rest, stage = refs[radix - 1 :]
    depth = pair_ref.shape[2]
    outer_rows(left_ref, right_refs, rest, product, order=order, rows=rows, **sizes)
    delta = dot(jnp.concatenate([first_ref[...], rest[...]], axis=0), table_ref[...])
    height = first_ref.shape[0]
    residues = height // (rows // 2)
    digit = me_ref[0] % radix
    mine = me_ref[0] // radix
    places = []
    for place in range(radix):
        value = delta[:height]
        for piece in range(1, radix):
            value = jnp.where(
                jnp.bitwise_xor(digit, piece) == place, delta[piece * height : (piece + 1) * height], value
            )
        places.append(value)
    group = rows * radix
    for row in range(rows):
        block = slice((row // 2) * residues, (row // 2 + 1) * residues)
        side = slice((row % 2) * depth, (row % 2 + 1) * depth)
        more = interleave([value[block, side] for value in places], rows)
        for at, step in enumerate(order):
            source = jnp.bitwise_xor(mine, step // radix)
            to = pl.ds(pl.multiple_of(source * group, group), group)
            stage[row, to, :] = more[at * group : (at + 1) * group]
        out_ref[row] = (pair_ref[row].astype(F32) + stage[row]).astype(BF16)


def interleave(parts, rows):
    total, lanes = parts[0].shape
    if rows != 4 or len(parts) != 2:
        return jnp.concatenate(
            [part[at : at + rows] for at in range(0, total, rows) for part in parts], axis=0
        )
    first, second = [part.reshape(total // 8, 8, lanes) for part in parts]
    upper = lax.broadcasted_iota(jnp.int32, first.shape, 1) < rows
    even = jnp.where(upper, first, pltpu.roll(second, rows, 1))
    odd = jnp.where(upper, pltpu.roll(first, rows, 1), second)
    return jnp.concatenate([even[:, None], odd[:, None]], axis=1).reshape(2 * total, lanes)


def gather_rounds(width):
    rounds = []
    stride = width
    while stride > 1:
        radix = 4 if stride % 4 == 0 else 2
        stride //= radix
        rounds.append([step * stride for step in reversed(range(1, radix))])
    return rounds


def gather_blocks(block, beside=()):
    width = lax.axis_size("dap")
    pieces = [block]
    order = [0]
    for at, steps in enumerate(gather_rounds(width)):
        stacked = jnp.concatenate(pieces, axis=0) if len(pieces) > 1 else pieces[0]
        if 0 < at <= len(beside):
            stacked, _ = lax.optimization_barrier((stacked, beside[at - 1]))
        pieces = [stacked]
        for step in steps:
            pieces.append(lax.ppermute(stacked, "dap", [(d, d ^ step) for d in range(width)]))
        order = order + [k ^ step for step in steps for k in order]
    return pieces, order


def per_device(
    homolog_features,
    twofold_features,
    twofold_offset_map,
    horizontal_attend_entry_maps,
    horizontal_attend_exit_map,
    vertical_attend_entry_maps,
    vertical_attend_exit_map,
    tensor_product_factors,
    tensor_product_exit_map,
):
    width = lax.axis_size("dap")
    sequences, residues, channels = homolog_features.shape
    rows, _, depth = twofold_features.shape
    heads = twofold_offset_map.shape[1]
    head_size = channels // heads
    groups = channels // LANES
    span = tensor_product_factors.shape[1] // 2
    count = sequences * width
    lanes = max(rows * span, LANES)
    tiles = channels // LANES

    me = lax.axis_index("dap").astype(jnp.int32).reshape(1)

    [halves] = call(
        functools.partial(bias_body, copies=width),
        [((width * heads * rows // 2, residues), BF16, False)],
        [twofold_features, twofold_offset_map.T],
        far=(0, 1),
    )
    features, halves = lax.optimization_barrier((homolog_features, halves))
    own = lax.all_to_all(halves, "dap", split_axis=0, concat_axis=0, tiled=True)
    kept, scores = call(
        functools.partial(row_scores_body, head_size=head_size),
        [
            ((groups, sequences * residues, 3 * LANES), BF16, True),
            ((sequences, groups, residues, LANES // head_size * residues), F32, True),
        ],
        [features, horizontal_attend_entry_maps],
        far=(0, 1),
        flops=10**9,
    )
    own, scores = lax.optimization_barrier((own, scores))
    other = lax.ppermute(own, "dap", [(d, d ^ 1) for d in range(width)])
    bias_scratch = [
        pltpu.VMEM((width * heads * rows // 2, residues), F32),
        pltpu.VMEM((heads // 2, residues, residues), F32),
    ]
    [gated] = call(
        functools.partial(row_first_body, blocks=width, head_size=head_size),
        [((groups // 2, sequences * residues, LANES), BF16, True)],
        [me, own, kept, scores],
        scratch=bias_scratch,
        flops=10**9,
    )
    [sent] = call(
        functools.partial(row_second_body, blocks=width, head_size=head_size),
        [((sequences * residues * tiles, LANES), BF16, True)],
        [me, other, kept, scores, gated, horizontal_attend_exit_map],
        scratch=bias_scratch + [pltpu.VMEM((sequences * residues * tiles, LANES), F32)],
    )
    received = lax.all_to_all(sent, "dap", split_axis=0, concat_axis=0, tiled=True)
    lines, left, right = call(
        functools.partial(column_body, rows=rows, head_size=head_size),
        [
            ((count * rows, channels), F32, True),
            ((lanes, count), BF16, True),
            ((rows * span, count), BF16, True),
        ],
        [received, vertical_attend_entry_maps, vertical_attend_exit_map, tensor_product_factors.T],
        scratch=[
            pltpu.VMEM((count * rows * tiles, LANES), F32),
            pltpu.VMEM((count * rows, 4 * channels), BF16),
            pltpu.VMEM((rows, groups, count, LANES // head_size * count), F32),
            pltpu.VMEM((rows * span, count), F32),
        ],
    )
    [table] = call(
        table_body,
        [((2 * span * span, 2 * depth), BF16, True)],
        [lax.optimization_barrier((tensor_product_exit_map, left))[0]],
        scratch=[pltpu.VMEM((span * span, depth), F32)],
        flops=10**9,
    )
    [alignment] = call(
        functools.partial(arrange_body, rows=rows),
        [((count * rows * tiles, LANES), BF16, False)],
        [lines],
        scratch=[pltpu.VMEM((count * rows * tiles, LANES), F32)],
        flops=10**9,
    )
    pieces, order = gather_blocks(right, (table, alignment))
    radix = len(pieces)
    sizes = dict(order=tuple(order[: width // radix]), span=span, count=count, rows=rows)
    share = residues // radix
    product = pltpu.VMEM((lanes // LANES, width // radix, rows * span, LANES), F32)
    height = rows // 2 * share
    [first] = call(
        functools.partial(outer_first_body, **sizes),
        [((height, 2 * span * span), BF16, True)],
        [left, pieces[0]],
        scratch=[product],
        flops=10**9,
    )
    [pair_output] = call(
        functools.partial(outer_last_body, radix=radix, **sizes),
        [(twofold_features.shape, BF16, False)],
        [me, left, *pieces[1:], table, first, twofold_features],
        scratch=[
            product,
            pltpu.VMEM(((radix - 1) * height, 2 * span * span), BF16),
            pltpu.VMEM((rows, residues, depth), F32),
        ],
    )
    alignment = alignment.reshape(count, tiles, rows, LANES).transpose(0, 2, 1, 3)
    return (alignment.reshape(count, rows, channels), pair_output)


def solution(mesh):
    in_specs = (
        P(("crop", "dap"), None, None),
        P(("crop", "dap"), None, None),
        P(),
        P(),
        P(),
        P(),
        P(),
        P(),
        P(),
    )
    out_specs = (P("crop", "dap", None), P(("crop", "dap"), None, None))
    return jax.shard_map(
        per_device, mesh=mesh, in_specs=in_specs, out_specs=out_specs, check_vma=False
    )
```

profile of v0, /device:TPU:0, one launch (start us, length us, event | category | flops | bytes accessed | tf_op | source)
XLA Modules:
  0.0 54.1 jit_solution(8343941370605515797)
XLA Ops:
  0.6 2.1 %shard_map.104 = bf16[512,128]{1,0:T(8,128)(2,1)} custom-call(bf16[4,128,128]{2,1,0:T(8,128)(2,1)} %refs_3_.1, bf16[8,128]{1,0:T(8,128)(2,1)} %bitcast.17), custom_call_target="tpu_custom_call" | custom-call | tf_op jit(solution)/shard_map/pallas_call | solution.py:36
  2.8 7.3 %all-to-all-start = ((bf16[32,16,128]{2,1,0:T(8,128)(2,1)}), bf16[32,16,128]{2,1,0:T(8,128)(2,1)S(1)}, u32[]{:S(2)}, u32[]{:S(2)}) async-start(bf16[32,16,128]{2,1,0:T(8,128)(2,1)} %bitcast.2), calls=%async_computation | async-start | bytes 262144 | tf_op jit(solution)/shard_map/all_to_all | solution.py:421
  10.1 2.1 %shard_map.105 = (bf16[2,512,384]{2,1,0:T(8,128)(2,1)S(1)}, f32[4,2,128,512]{3,2,1,0:T(8,128)S(1)}) custom-call(bf16[4,128,256]{2,1,0:T(8,128)(2,1)} %features_ref, bf16[256,1024]{1,0:T(8,128)(2,1)} %maps_ref.2), custom_call_target="tpu_custom_call" | custom-call | flops 1000000000 | tf_op jit(solution)/shard_map/pallas_call | solution.py:36
  12.2 0.0 copy-start.3
  12.2 6.1 %all-to-all-done = bf16[32,16,128]{2,1,0:T(8,128)(2,1)S(1)} async-done(((bf16[32,16,128]{2,1,0:T(8,128)(2,1)}), bf16[32,16,128]{2,1,0:T(8,128)(2,1)S(1)}, u32[]{:S(2)}, u32[]{:S(2)}) %all-to-all-start) | async-done | bytes 131104 | tf_op jit(solution)/shard_map/all_to_all | solution.py:421
  18.3 0.2 collective-permute-start
  18.5 0.5 shard_map.106.gated_ref
  19.0 0.0 copy-start
  19.1 0.0 copy-start.2
  19.1 0.0 copy-start.4
  19.1 0.0 copy-start.5
  19.1 0.6 %collective-permute-done.bias_ref = bf16[512,128]{1,0:T(8,128)(2,1)S(1)} collective-permute-done((bf16[512,128]{1,0:T(8,128)(2,1)S(1)}, bf16[512,128]{1,0:T(8,128)(2,1)S(1)}, u32[]{:S(2)}, u32[]{:S(2)}) %collective-permute-start) | collective-permute-done | bytes 131104 | tf_op jit(solution)/shard_map/ppermute | solution.py:433
  19.7 0.0 copy-done.3
  19.7 0.7 %shard_map.107 = bf16[1024,128]{1,0:T(8,128)(2,1)S(1)} custom-call(s32[1]{0:T(128)} %bitcast.me_ref, bf16[512,128]{1,0:T(8,128)(2,1)S(1)} %collective-permute-done.bias_ref, bf16[2,512,384]{2,1,0:T(8,128)(2,1)S(1)} %get-tuple-element.18.kept_ref, f32[4,2,128,512]{3,2,1,0:T(8,128)S(1)} %get-tuple-element.19.scores_ref, ...), custom_call_target="tpu_custom_call" | custom-call | tf_op jit(solution)/shard_map/pallas_call | solution.py:36
  20.4 12.3 %all_to_all.23 = bf16[32,32,128]{2,1,0:T(8,128)(2,1)S(1)} all-to-all(bf16[32,32,128]{2,1,0:T(8,128)(2,1)S(1)} %bitcast.13), channel_id=1, replica_groups=mesh['crop'=1,'dap'=32] {'dap'}, dimensions={0} | all-to-all | bytes 524288 | tf_op jit(solution)/shard_map/all_to_all | solution.py:451
  32.7 0.0 copy-done
  32.7 0.0 copy-done.2
  32.7 0.0 copy-done.4
  32.7 2.1 %shard_map.108 = (f32[512,256]{1,0:T(8,128)S(1)}, bf16[128,128]{1,0:T(8,128)(2,1)S(1)}, bf16[128,128]{1,0:T(8,128)(2,1)S(1)}) custom-call(bf16[1024,128]{1,0:T(8,128)(2,1)S(1)} %bitcast.12, bf16[256,1024]{1,0:T(8,128)(2,1)S(1)} %copy-done, bf16[256,256]{1,0:T(8,128)(2,1)S(1)} %copy-done.2, bf16[64,256]{1,0:T(8,128)(2,1)S(1)} %bitcast.16), custom_call_target="tpu_custom_call" | custom-call | tf_op jit(solution)/shard_map/pallas_call | solution.py:36
  34.9 1.0 %collective-permute-start.3 = (bf16[128,128]{1,0:T(8,128)(2,1)S(1)}, bf16[128,128]{1,0:T(8,128)(2,1)S(1)}, u32[]{:S(2)}, u32[]{:S(2)}) collective-permute-start(bf16[128,128]{1,0:T(8,128)(2,1)S(1)} %get-tuple-element.22), channel_id=1, source_target_pairs={{0,8},{1,9},{2,10},{3,11},{4,12},{5,13},{6,14},{7,15},{8,0},{9,1},... | collective-permute-start | bytes 98312 | tf_op jit(solution)/shard_map/ppermute | solution.py:385
  35.8 1.0 %collective-permute-start.2 = (bf16[128,128]{1,0:T(8,128)(2,1)S(1)}, bf16[128,128]{1,0:T(8,128)(2,1)S(1)}, u32[]{:S(2)}, u32[]{:S(2)}) collective-permute-start(bf16[128,128]{1,0:T(8,128)(2,1)S(1)} %get-tuple-element.22), channel_id=1, source_target_pairs={{0,16},{1,17},{2,18},{3,19},{4,20},{5,21},{6,22},{7,23},{8,24},{9,... | collective-permute-start | bytes 98312 | tf_op jit(solution)/shard_map/ppermute | solution.py:385
  36.8 2.5 %collective-permute-start.1 = (bf16[128,128]{1,0:T(8,128)(2,1)S(1)}, bf16[128,128]{1,0:T(8,128)(2,1)S(1)}, u32[]{:S(2)}, u32[]{:S(2)}) collective-permute-start(bf16[128,128]{1,0:T(8,128)(2,1)S(1)} %get-tuple-element.22), channel_id=1, source_target_pairs={{0,24},{1,25},{2,26},{3,27},{4,28},{5,29},{6,30},{7,31},{8,16},{9,... | collective-permute-start | bytes 98312 | tf_op jit(solution)/shard_map/ppermute | solution.py:385
  39.3 0.0 copy-done.5
  39.3 0.3 shard_map.110.refs_1_
  39.7 0.0 collective-permute-done.3
  39.7 1.7 %collective-permute-done.2 = bf16[128,128]{1,0:T(8,128)(2,1)S(1)} collective-permute-done((bf16[128,128]{1,0:T(8,128)(2,1)S(1)}, bf16[128,128]{1,0:T(8,128)(2,1)S(1)}, u32[]{:S(2)}, u32[]{:S(2)}) %collective-permute-start.2) | collective-permute-done | bytes 32800 | tf_op jit(solution)/shard_map/ppermute | solution.py:385
  41.4 1.2 %collective-permute-done.1 = bf16[128,128]{1,0:T(8,128)(2,1)S(1)} collective-permute-done((bf16[128,128]{1,0:T(8,128)(2,1)S(1)}, bf16[128,128]{1,0:T(8,128)(2,1)S(1)}, u32[]{:S(2)}, u32[]{:S(2)}) %collective-permute-start.1) | collective-permute-done | bytes 32800 | tf_op jit(solution)/shard_map/ppermute | solution.py:385
  42.5 0.6 %collective-permute-start.6 = (bf16[512,128]{1,0:T(8,128)(2,1)S(1)}, bf16[512,128]{1,0:T(8,128)(2,1)S(1)}, u32[]{:S(2)}, u32[]{:S(2)}) collective-permute-start(bf16[512,128]{1,0:T(8,128)(2,1)S(1)} %pad_maximum_fusion.1), channel_id=1, source_target_pairs={{0,2},{1,3},{2,0},{3,1},{4,6},{5,7},{6,4},{7,5},{8,10},{9,11},{10,... | collective-permute-start | bytes 393224 | tf_op jit(solution)/shard_map/ppermute | solution.py:385
  43.2 1.3 %collective-permute-start.5 = (bf16[512,128]{1,0:T(8,128)(2,1)S(1)}, bf16[512,128]{1,0:T(8,128)(2,1)S(1)}, u32[]{:S(2)}, u32[]{:S(2)}) collective-permute-start(bf16[512,128]{1,0:T(8,128)(2,1)S(1)} %pad_maximum_fusion.1), channel_id=1, source_target_pairs={{0,4},{1,5},{2,6},{3,7},{4,0},{5,1},{6,2},{7,3},{8,12},{9,13},{10,... | collective-permute-start | bytes 393224 | tf_op jit(solution)/shard_map/ppermute | solution.py:385
  44.4 1.7 %collective-permute-start.4 = (bf16[512,128]{1,0:T(8,128)(2,1)S(1)}, bf16[512,128]{1,0:T(8,128)(2,1)S(1)}, u32[]{:S(2)}, u32[]{:S(2)}) collective-permute-start(bf16[512,128]{1,0:T(8,128)(2,1)S(1)} %pad_maximum_fusion.1), channel_id=1, source_target_pairs={{0,6},{1,7},{2,4},{3,5},{4,2},{5,3},{6,0},{7,1},{8,14},{9,15},{10,... | collective-permute-start | bytes 393224 | tf_op jit(solution)/shard_map/ppermute | solution.py:385
  46.1 0.9 %shard_map.109 = bf16[1024,128]{1,0:T(8,128)(2,1)} custom-call(f32[512,256]{1,0:T(8,128)S(1)} %get-tuple-element.20.lines_ref), custom_call_target="tpu_custom_call" | custom-call | flops 1000000000 | tf_op jit(solution)/shard_map/pallas_call | solution.py:36
  47.0 1.0 %collective-permute-done.6 = bf16[512,128]{1,0:T(8,128)(2,1)S(1)} collective-permute-done((bf16[512,128]{1,0:T(8,128)(2,1)S(1)}, bf16[512,128]{1,0:T(8,128)(2,1)S(1)}, u32[]{:S(2)}, u32[]{:S(2)}) %collective-permute-start.6) | collective-permute-done | bytes 131104 | tf_op jit(solution)/shard_map/ppermute | solution.py:385
  48.0 0.5 collective-permute-done.5
  48.5 1.8 %collective-permute-done.4 = bf16[512,128]{1,0:T(8,128)(2,1)S(1)} collective-permute-done((bf16[512,128]{1,0:T(8,128)(2,1)S(1)}, bf16[512,128]{1,0:T(8,128)(2,1)S(1)}, u32[]{:S(2)}, u32[]{:S(2)}) %collective-permute-start.4) | collective-permute-done | bytes 131104 | tf_op jit(solution)/shard_map/ppermute | solution.py:385
  50.4 0.0 copy-start.1
  50.4 0.1 collective-permute-start.7
  50.4 0.5 shard_map.111.refs_2_
  51.0 1.4 %collective-permute-done.7.refs_0_ = bf16[2048,128]{1,0:T(8,128)(2,1)S(1)} collective-permute-done((bf16[2048,128]{1,0:T(8,128)(2,1)S(1)}, bf16[2048,128]{1,0:T(8,128)(2,1)S(1)}, u32[]{:S(2)}, u32[]{:S(2)}) %collective-permute-start.7) | collective-permute-done | bytes 524320 | tf_op jit(solution)/shard_map/ppermute | solution.py:385
  52.3 0.0 copy-done.1
  52.3 1.7 %shard_map.112 = bf16[4,128,128]{2,1,0:T(8,128)(2,1)} custom-call(s32[1]{0:T(128)} %bitcast.me_ref, bf16[128,128]{1,0:T(8,128)(2,1)S(1)} %get-tuple-element.21.left_ref, bf16[2048,128]{1,0:T(8,128)(2,1)S(1)} %collective-permute-done.7.refs_0_, bf16[2048,256]{1,0:T(8,128)(2,1)S(1)} %shard_map.110.refs_1_, bf16[128,2048]{1,0:T(8,128)(2,1)S(1)} %shard_map.111.refs_2_, ...), custom_call_target="tpu_custom_call" | custom-call | tf_op jit(solution)/shard_map/pallas_call | solution.py:36
  (2 shorter events, 0.0 us)
Async XLA Ops:
  2.8 15.5 %all-to-all-start = ((bf16[32,16,128]{2,1,0:T(8,128)(2,1)}), bf16[32,16,128]{2,1,0:T(8,128)(2,1)S(1)}, u32[]{:S(2)}, u32[]{:S(2)}) async-start(bf16[32,16,128]{2,1,0:T(8,128)(2,1)} %bitcast.2), calls=%async_computation | async-start | bytes 262144 | tf_op jit(solution)/shard_map/all_to_all | solution.py:421
  12.2 7.5 %copy-start.3 = (bf16[256,256]{1,0:T(8,128)(2,1)S(1)}, bf16[256,256]{1,0:T(8,128)(2,1)}, u32[]{:S(2)}) copy-start(bf16[256,256]{1,0:T(8,128)(2,1)} %exit_ref.2) | copy-start | bytes 393220
  18.3 1.3 %collective-permute-start = (bf16[512,128]{1,0:T(8,128)(2,1)S(1)}, bf16[512,128]{1,0:T(8,128)(2,1)S(1)}, u32[]{:S(2)}, u32[]{:S(2)}) collective-permute-start(bf16[512,128]{1,0:T(8,128)(2,1)S(1)} %bitcast.14), channel_id=1, source_target_pairs={{0,1},{1,0},{2,3},{3,2},{4,5},{5,4},{6,7},{7,6},{8,9},{9,8},{10,11... | collective-permute-start | bytes 393224 | tf_op jit(solution)/shard_map/ppermute | solution.py:433
  19.0 13.7 %copy-start = (bf16[256,1024]{1,0:T(8,128)(2,1)S(1)}, bf16[256,1024]{1,0:T(8,128)(2,1)}, u32[]{:S(2)}) copy-start(bf16[256,1024]{1,0:T(8,128)(2,1)} %maps_ref.3) | copy-start | bytes 1572868
  19.1 13.7 %copy-start.2 = (bf16[256,256]{1,0:T(8,128)(2,1)S(1)}, bf16[256,256]{1,0:T(8,128)(2,1)}, u32[]{:S(2)}) copy-start(bf16[256,256]{1,0:T(8,128)(2,1)} %exit_ref.3) | copy-start | bytes 393220
  19.1 13.6 %copy-start.4 = (bf16[256,64]{0,1:T(8,128)(2,1)S(1)}, bf16[256,64]{0,1:T(8,128)(2,1)}, u32[]{:S(2)}) copy-start(bf16[256,64]{0,1:T(8,128)(2,1)} %param.16) | copy-start | bytes 98308
  19.1 20.2 %copy-start.5 = (bf16[1024,128]{1,0:T(8,128)(2,1)S(1)}, bf16[1024,128]{1,0:T(8,128)(2,1)}, u32[]{:S(2)}) copy-start(bf16[1024,128]{1,0:T(8,128)(2,1)} %exit_ref.4) | copy-start | bytes 786436
  34.9 4.8 %collective-permute-start.3 = (bf16[128,128]{1,0:T(8,128)(2,1)S(1)}, bf16[128,128]{1,0:T(8,128)(2,1)S(1)}, u32[]{:S(2)}, u32[]{:S(2)}) collective-permute-start(bf16[128,128]{1,0:T(8,128)(2,1)S(1)} %get-tuple-element.22), channel_id=1, source_target_pairs={{0,8},{1,9},{2,10},{3,11},{4,12},{5,13},{6,14},{7,15},{8,0},{9,1},... | collective-permute-start | bytes 98312 | tf_op jit(solution)/shard_map/ppermute | solution.py:385
  35.8 5.5 %collective-permute-start.2 = (bf16[128,128]{1,0:T(8,128)(2,1)S(1)}, bf16[128,128]{1,0:T(8,128)(2,1)S(1)}, u32[]{:S(2)}, u32[]{:S(2)}) collective-permute-start(bf16[128,128]{1,0:T(8,128)(2,1)S(1)} %get-tuple-element.22), channel_id=1, source_target_pairs={{0,16},{1,17},{2,18},{3,19},{4,20},{5,21},{6,22},{7,23},{8,24},{9,... | collective-permute-start | bytes 98312 | tf_op jit(solution)/shard_map/ppermute | solution.py:385
  36.8 5.7 %collective-permute-start.1 = (bf16[128,128]{1,0:T(8,128)(2,1)S(1)}, bf16[128,128]{1,0:T(8,128)(2,1)S(1)}, u32[]{:S(2)}, u32[]{:S(2)}) collective-permute-start(bf16[128,128]{1,0:T(8,128)(2,1)S(1)} %get-tuple-element.22), channel_id=1, source_target_pairs={{0,24},{1,25},{2,26},{3,27},{4,28},{5,29},{6,30},{7,31},{8,16},{9,... | collective-permute-start | bytes 98312 | tf_op jit(solution)/shard_map/ppermute | solution.py:385
  42.5 5.5 %collective-permute-start.6 = (bf16[512,128]{1,0:T(8,128)(2,1)S(1)}, bf16[512,128]{1,0:T(8,128)(2,1)S(1)}, u32[]{:S(2)}, u32[]{:S(2)}) collective-permute-start(bf16[512,128]{1,0:T(8,128)(2,1)S(1)} %pad_maximum_fusion.1), channel_id=1, source_target_pairs={{0,2},{1,3},{2,0},{3,1},{4,6},{5,7},{6,4},{7,5},{8,10},{9,11},{10,... | collective-permute-start | bytes 393224 | tf_op jit(solution)/shard_map/ppermute | solution.py:385
  43.2 5.3 %collective-permute-start.5 = (bf16[512,128]{1,0:T(8,128)(2,1)S(1)}, bf16[512,128]{1,0:T(8,128)(2,1)S(1)}, u32[]{:S(2)}, u32[]{:S(2)}) collective-permute-start(bf16[512,128]{1,0:T(8,128)(2,1)S(1)} %pad_maximum_fusion.1), channel_id=1, source_target_pairs={{0,4},{1,5},{2,6},{3,7},{4,0},{5,1},{6,2},{7,3},{8,12},{9,13},{10,... | collective-permute-start | bytes 393224 | tf_op jit(solution)/shard_map/ppermute | solution.py:385
  44.4 5.9 %collective-permute-start.4 = (bf16[512,128]{1,0:T(8,128)(2,1)S(1)}, bf16[512,128]{1,0:T(8,128)(2,1)S(1)}, u32[]{:S(2)}, u32[]{:S(2)}) collective-permute-start(bf16[512,128]{1,0:T(8,128)(2,1)S(1)} %pad_maximum_fusion.1), channel_id=1, source_target_pairs={{0,6},{1,7},{2,4},{3,5},{4,2},{5,3},{6,0},{7,1},{8,14},{9,15},{10,... | collective-permute-start | bytes 393224 | tf_op jit(solution)/shard_map/ppermute | solution.py:385
  50.4 2.0 %copy-start.1 = (bf16[4,128,128]{2,1,0:T(8,128)(2,1)S(1)}, bf16[4,128,128]{2,1,0:T(8,128)(2,1)}, u32[]{:S(2)}) copy-start(bf16[4,128,128]{2,1,0:T(8,128)(2,1)} %refs_3_.1) | copy-start | bytes 393220
  50.4 2.0 %collective-permute-start.7 = (bf16[2048,128]{1,0:T(8,128)(2,1)S(1)}, bf16[2048,128]{1,0:T(8,128)(2,1)S(1)}, u32[]{:S(2)}, u32[]{:S(2)}) collective-permute-start(bf16[2048,128]{1,0:T(8,128)(2,1)S(1)} %pad_maximum_fusion.right_ref), channel_id=1, source_target_pairs={{0,1},{1,0},{2,3},{3,2},{4,5},{5,4},{6,7},{7,6},{8,9},{9,8},{10,11... | collective-permute-start | bytes 1572872 | tf_op jit(solution)/shard_map/ppermute | solution.py:385
where the time goes:
time: 54.3 us; the launch traced here: 54.1 us
  starting transfers between devices  15.6 us (29%)
  waiting for transfers between devices  14.2 us (26%)
  blocking collectives  12.3 us (23%)
  Pallas kernels  11.1 us (20%)
  between operations  0.76 us (1%)
    all_to_all x1, blocking collectives, per_device(): lax.all_to_all(sent, 'dap', split_axis=0, concat_axis=0, tiled=True)  12.3 us
    pallas_call x9, Pallas kernels, call(): pl.pallas_call(body, out_shape=[pltpu.VMEM(shape, dtype) if near else jax...  11.1 us
    ppermute x7, starting transfers between devices, gather_blocks(): lax.ppermute(stacked, 'dap', [(d, d ^ step) for d in range(width)])  8.08 us
    ppermute x7, waiting for transfers between devices, gather_blocks(): lax.ppermute(stacked, 'dap', [(d, d ^ step) for d in range(width)])  7.56 us
    all_to_all x1, starting transfers between devices, per_device(): own = lax.all_to_all(halves, 'dap', split_axis=0, concat_axis=0, tiled=True)  7.33 us
    all_to_all x1, waiting for transfers between devices, per_device(): own = lax.all_to_all(halves, 'dap', split_axis=0, concat_axis=0, tiled=True)  6.11 us
  transfers between devices with their start and end apart: 9, of which 8 were waited for; matrix products, arithmetic and copies ran while one was open for 0% of the time, Pallas kernels for 8%

commit v1 on v0

--- a/solution.py
+++ b/solution.py
@@ -11,6 +11,7 @@
 
 EPSILON = 1e-05
 LANES = 128
+LOG2_E = math.log2(math.e)
 F32 = jnp.float32
 BF16 = jnp.bfloat16
 VMEM = pl.BlockSpec(memory_space=pltpu.VMEM)
@@ -82,14 +83,20 @@
         out_ref[copy * half : (copy + 1) * half, :] = block[copy % 2 * half : (copy % 2 + 1) * half, :]
 
 
-def scores_of(proj, head_size, masks):
+def project(values, maps, head_size):
+    width = maps.shape[1] // 4
+    proj = dot(standardize(values), maps)
+    queries = proj[:, :width] * (LOG2_E / math.sqrt(head_size))
+    return jnp.concatenate([queries, proj[:, width:]], axis=1).astype(BF16)
+
+
+def scores_of(proj, masks):
     width = proj.shape[1] // 4
-    scale = 1.0 / math.sqrt(head_size)
     scores = []
     for start in range(0, width, LANES):
         queries = proj[:, start : start + LANES]
         keys = masked_rows(proj[:, width + start : width + start + LANES], masks)
-        scores.append(dot_t(queries, keys) * scale)
+        scores.append(dot_t(queries, keys))
     return scores
 
 
@@ -99,7 +106,7 @@
     for at in range(len(masks)):
         piece = scores[at]
         highest = jnp.max(piece, axis=-1, keepdims=True)
-        pieces.append(jnp.exp(piece - highest).astype(BF16))
+        pieces.append(jnp.exp2(piece - highest).astype(BF16))
     ones = jnp.ones((keys, LANES), BF16)
     table = jnp.concatenate([masked_rows(values, masks), masked_rows(ones, masks)], axis=1)
     sums = dot(jnp.concatenate(pieces, axis=1), table)
@@ -110,7 +117,7 @@
 def row_scores_body(features_ref, maps_ref, kept_ref, scores_ref, *, head_size):
     sequences, residues, channels = features_ref.shape
     features = features_ref[...].reshape(sequences * residues, channels)
-    proj = dot(standardize(features.astype(F32)), maps_ref[...]).astype(BF16)
+    proj = project(features.astype(F32), maps_ref[...], head_size)
     for block, start in enumerate(range(0, channels, LANES)):
         kept_ref[block, :, :LANES] = proj[:, 2 * channels + start : 2 * channels + start + LANES]
         kept_ref[block, :, LANES : 2 * LANES] = proj[:, 3 * channels + start : 3 * channels + start + LANES]
@@ -118,7 +125,7 @@
     masks = lane_masks(head_size, residues)
     for at in range(sequences):
         mine = proj[at * residues : (at + 1) * residues, :]
-        for block, scores in enumerate(scores_of(mine, head_size, masks)):
+        for block, scores in enumerate(scores_of(mine, masks)):
             scores_ref[at, block] = scores
 
 
@@ -127,7 +134,7 @@
     rows = residues // blocks
     heads = bias_ref.shape[0] // residues
     masks = lane_masks(head_size, residues)
-    wide[...] = bias_ref[...].astype(F32)
+    wide[...] = bias_ref[...].astype(F32) * LOG2_E
     for source in range(blocks):
         for head in range(heads):
             start = (source * heads + head) * rows
@@ -149,43 +156,42 @@
     return gated
 
 
-def row_first_body(me_ref, bias_ref, kept_ref, scores_ref, out_ref, wide, bias, *, blocks, head_size):
-    groups = kept_ref.shape[0] // 2
-    residues = scores_ref.shape[2]
-    first = jnp.bitwise_and(me_ref[0], 1) * groups
+def exit_share(gated, exit_ref, first, at):
+    delta = None
+    for block, parts in enumerate(gated):
+        rows = pl.ds(pl.multiple_of((first + block) * LANES, LANES), LANES)
+        more = dot(parts[at], exit_ref[rows, :])
+        delta = more if delta is None else delta + more
+    return delta
+
+
+def row_first_body(me_ref, bias_ref, kept_ref, scores_ref, exit_ref, out_ref, wide, bias, *, blocks, head_size):
+    sequences, tiles, residues, _ = scores_ref.shape
+    first = jnp.bitwise_and(me_ref[0], 1) * (tiles // 2)
     gated = row_half(bias_ref, kept_ref, scores_ref, wide, bias, first, blocks, head_size)
-    for block, parts in enumerate(gated):
-        for at, part in enumerate(parts):
-            out_ref[block, at * residues : (at + 1) * residues, :] = part
+    for at in range(sequences):
+        mine = slice(at * residues, (at + 1) * residues)
+        delta = exit_share(gated, exit_ref, first, at)
+        for tile in range(tiles):
+            side = slice(tile * LANES, (tile + 1) * LANES)
+            out_ref[mine, side] = kept_ref[tile, mine, 2 * LANES :].astype(F32) + delta[:, side]
 
 
 def row_second_body(
-    me_ref, bias_ref, kept_ref, scores_ref, gated_ref, exit_ref, out_ref, wide, bias, sent, *, blocks, head_size
+    me_ref, bias_ref, kept_ref, scores_ref, exit_ref, lines_ref, out_ref, wide, bias, sent, *, blocks, head_size
 ):
-    groups = kept_ref.shape[0] // 2
     sequences, tiles, residues, _ = scores_ref.shape
     rows = residues // blocks
-    parity = jnp.bitwise_and(me_ref[0], 1)
-    gated = row_half(bias_ref, kept_ref, scores_ref, wide, bias, (1 - parity) * groups, blocks, head_size)
-
-    def exit_rows(group):
-        return exit_ref[pl.ds(pl.multiple_of(group * LANES, LANES), LANES), :]
-
+    first = (1 - jnp.bitwise_and(me_ref[0], 1)) * (tiles // 2)
+    gated = row_half(bias_ref, kept_ref, scores_ref, wide, bias, first, blocks, head_size)
     for at in range(sequences):
-        mine = slice(at * residues, (at + 1) * residues)
-        delta = None
-        for block in range(groups):
-            for part, group in (
-                (gated_ref[block, mine, :], parity * groups + block),
-                (gated[block][at], (1 - parity) * groups + block),
-            ):
-                more = dot(part, exit_rows(group))
-                delta = more if delta is None else delta + more
+        line = lines_ref[at * residues : (at + 1) * residues, :] + exit_share(gated, exit_ref, first, at)
         for tile in range(tiles):
-            line = kept_ref[tile, mine, 2 * LANES :].astype(F32) + delta[:, tile * LANES : (tile + 1) * LANES]
             for target in range(blocks):
                 start = ((target * sequences + at) * tiles + tile) * rows
-                sent[start : start + rows, :] = line[target * rows : (target + 1) * rows, :]
+                sent[start : start + rows, :] = line[
+                    target * rows : (target + 1) * rows, tile * LANES : (tile + 1) * LANES
+                ]
     out_ref[...] = sent[...].astype(BF16)
 
 
@@ -208,10 +214,10 @@
     lines = jnp.concatenate(
         [jnp.concatenate([wide[rows_of, :] for rows_of in one], axis=1) for one in chosen], axis=0
     )
-    proj_ref[...] = dot(standardize(lines), maps_ref[...]).astype(BF16)
+    proj_ref[...] = project(lines, maps_ref[...], head_size)
     for at in range(rows):
         proj = proj_ref[at * sequences : (at + 1) * sequences, :]
-        for block, scores in enumerate(scores_of(proj, head_size, masks)):
+        for block, scores in enumerate(scores_of(proj, masks)):
             score_ref[at, block] = scores
     gated = []
     for at in range(rows):
@@ -435,17 +441,17 @@
         pltpu.VMEM((width * heads * rows // 2, residues), F32),
         pltpu.VMEM((heads // 2, residues, residues), F32),
     ]
-    [gated] = call(
+    [lines] = call(
         functools.partial(row_first_body, blocks=width, head_size=head_size),
-        [((groups // 2, sequences * residues, LANES), BF16, True)],
-        [me, own, kept, scores],
+        [((sequences * residues, channels), F32, True)],
+        [me, own, kept, scores, horizontal_attend_exit_map],
         scratch=bias_scratch,
         flops=10**9,
     )
     [sent] = call(
         functools.partial(row_second_body, blocks=width, head_size=head_size),
         [((sequences * residues * tiles, LANES), BF16, True)],
-        [me, other, kept, scores, gated, horizontal_attend_exit_map],
+        [me, other, kept, scores, horizontal_attend_exit_map, lines],
         scratch=bias_scratch + [pltpu.VMEM((sequences * residues * tiles, LANES), F32)],
     )
     received = lax.all_to_all(sent, "dap", split_axis=0, concat_axis=0, tiled=True)

time: 54.3 us -> 54.2 us (level)
  no operation moved by 1% of the time
where the time goes in v1:
time: 54.2 us; the launch traced here: 54 us
  starting transfers between devices  15.6 us (29%)
  waiting for transfers between devices  14.1 us (26%)
  blocking collectives  12.3 us (23%)
  Pallas kernels  11.1 us (20%)
  between operations  0.75 us (1%)
    all_to_all x1, blocking collectives, per_device(): lax.all_to_all(sent, 'dap', split_axis=0, concat_axis=0, tiled=True)  12.3 us
    pallas_call x9, Pallas kernels, call(): pl.pallas_call(body, out_shape=[pltpu.VMEM(shape, dtype) if near else jax...  11.1 us
    ppermute x7, starting transfers between devices, gather_blocks(): lax.ppermute(stacked, 'dap', [(d, d ^ step) for d in range(width)])  8.08 us
    ppermute x7, waiting for transfers between devices, gather_blocks(): lax.ppermute(stacked, 'dap', [(d, d ^ step) for d in range(width)])  7.57 us
    all_to_all x1, starting transfers between devices, per_device(): own = lax.all_to_all(halves, 'dap', split_axis=0, concat_axis=0, tiled=True)  7.33 us
    all_to_all x1, waiting for transfers between devices, per_device(): own = lax.all_to_all(halves, 'dap', split_axis=0, concat_axis=0, tiled=True)  6.12 us
  transfers between devices with their start and end apart: 9, of which 8 were waited for; matrix products, arithmetic and copies ran while one was open for 0% of the time, Pallas kernels for 8%

profile of v1, /device:TPU:0, one launch (start us, length us, event | category | flops | bytes accessed | tf_op | source)
XLA Modules:
  0.0 54.0 jit_solution(99078161311834036)
XLA Ops:
  0.6 0.0 copy-start.2
  0.6 2.2 %shard_map.104 = bf16[512,128]{1,0:T(8,128)(2,1)} custom-call(bf16[4,128,128]{2,1,0:T(8,128)(2,1)} %refs_3_.1, bf16[8,128]{1,0:T(8,128)(2,1)} %bitcast.17), custom_call_target="tpu_custom_call" | custom-call | tf_op jit(solution)/shard_map/pallas_call | solution.py:37
  2.8 7.3 %all-to-all-start = ((bf16[32,16,128]{2,1,0:T(8,128)(2,1)}), bf16[32,16,128]{2,1,0:T(8,128)(2,1)S(1)}, u32[]{:S(2)}, u32[]{:S(2)}) async-start(bf16[32,16,128]{2,1,0:T(8,128)(2,1)} %bitcast.2), calls=%async_computation | async-start | bytes 262144 | tf_op jit(solution)/shard_map/all_to_all | solution.py:427
  10.1 2.1 %shard_map.105 = (bf16[2,512,384]{2,1,0:T(8,128)(2,1)S(1)}, f32[4,2,128,512]{3,2,1,0:T(8,128)S(1)}) custom-call(bf16[4,128,256]{2,1,0:T(8,128)(2,1)} %features_ref, bf16[256,1024]{1,0:T(8,128)(2,1)} %maps_ref.2), custom_call_target="tpu_custom_call" | custom-call | flops 1000000000 | tf_op jit(solution)/shard_map/pallas_call | solution.py:37
  12.2 6.1 %all-to-all-done = bf16[32,16,128]{2,1,0:T(8,128)(2,1)S(1)} async-done(((bf16[32,16,128]{2,1,0:T(8,128)(2,1)}), bf16[32,16,128]{2,1,0:T(8,128)(2,1)S(1)}, u32[]{:S(2)}, u32[]{:S(2)}) %all-to-all-start) | async-done | bytes 131104 | tf_op jit(solution)/shard_map/all_to_all | solution.py:427
  18.4 0.2 collective-permute-start
  18.6 0.0 copy-done.2
  18.6 0.6 %shard_map.106.lines_ref = f32[512,256]{1,0:T(8,128)S(1)} custom-call(s32[1]{0:T(128)} %bitcast.me_ref, bf16[512,128]{1,0:T(8,128)(2,1)S(1)} %bitcast.15, bf16[2,512,384]{2,1,0:T(8,128)(2,1)S(1)} %get-tuple-element.18.kept_ref, f32[4,2,128,512]{3,2,1,0:T(8,128)S(1)} %get-tuple-element.19.scores_ref, bf16[256,256]{1,0:T(8,128)(2,1)S(1)} %copy-done.2), custom_call_target="tpu_custom_call" | custom-call | flops 1000000000 | tf_op jit(solution)/shard_map/pallas_call | solution.py:37
  19.2 0.0 copy-start
  19.2 0.0 copy-start.3
  19.2 0.0 copy-start.4
  19.3 0.0 copy-start.5
  19.3 0.4 collective-permute-done.bias_ref
  19.7 0.7 %shard_map.107 = bf16[1024,128]{1,0:T(8,128)(2,1)S(1)} custom-call(s32[1]{0:T(128)} %bitcast.me_ref, bf16[512,128]{1,0:T(8,128)(2,1)S(1)} %collective-permute-done.bias_ref, bf16[2,512,384]{2,1,0:T(8,128)(2,1)S(1)} %get-tuple-element.18.kept_ref, f32[4,2,128,512]{3,2,1,0:T(8,128)S(1)} %get-tuple-element.19.scores_ref, bf16[256,256]{1,0:T(8,128)(2,1)S(1)} %copy-done.2, ...), custom_call_target="tpu_custom_call" | custom-call | tf_op jit(solution)/shard_map/pallas_call | solution.py:37
  20.4 12.3 %all_to_all.23 = bf16[32,32,128]{2,1,0:T(8,128)(2,1)S(1)} all-to-all(bf16[32,32,128]{2,1,0:T(8,128)(2,1)S(1)} %bitcast.12), channel_id=1, replica_groups=mesh['crop'=1,'dap'=32] {'dap'}, dimensions={0} | all-to-all | bytes 524288 | tf_op jit(solution)/shard_map/all_to_all | solution.py:457
  32.7 0.0 copy-done
  32.7 0.0 copy-done.3
  32.7 0.0 copy-done.4
  32.7 2.0 %shard_map.108 = (f32[512,256]{1,0:T(8,128)S(1)}, bf16[128,128]{1,0:T(8,128)(2,1)S(1)}, bf16[128,128]{1,0:T(8,128)(2,1)S(1)}) custom-call(bf16[1024,128]{1,0:T(8,128)(2,1)S(1)} %bitcast.13, bf16[256,1024]{1,0:T(8,128)(2,1)S(1)} %copy-done, bf16[256,256]{1,0:T(8,128)(2,1)S(1)} %copy-done.3, bf16[64,256]{1,0:T(8,128)(2,1)S(1)} %bitcast.16), custom_call_target="tpu_custom_call" | custom-call | tf_op jit(solution)/shard_map/pallas_call | solution.py:37
  34.8 1.0 %collective-permute-start.3 = (bf16[128,128]{1,0:T(8,128)(2,1)S(1)}, bf16[128,128]{1,0:T(8,128)(2,1)S(1)}, u32[]{:S(2)}, u32[]{:S(2)}) collective-permute-start(bf16[128,128]{1,0:T(8,128)(2,1)S(1)} %get-tuple-element.22), channel_id=1, source_target_pairs={{0,8},{1,9},{2,10},{3,11},{4,12},{5,13},{6,14},{7,15},{8,0},{9,1},... | collective-permute-start | bytes 98312 | tf_op jit(solution)/shard_map/ppermute | solution.py:391
  35.8 1.0 %collective-permute-start.2 = (bf16[128,128]{1,0:T(8,128)(2,1)S(1)}, bf16[128,128]{1,0:T(8,128)(2,1)S(1)}, u32[]{:S(2)}, u32[]{:S(2)}) collective-permute-start(bf16[128,128]{1,0:T(8,128)(2,1)S(1)} %get-tuple-element.22), channel_id=1, source_target_pairs={{0,16},{1,17},{2,18},{3,19},{4,20},{5,21},{6,22},{7,23},{8,24},{9,... | collective-permute-start | bytes 98312 | tf_op jit(solution)/shard_map/ppermute | solution.py:391
  36.7 2.5 %collective-permute-start.1 = (bf16[128,128]{1,0:T(8,128)(2,1)S(1)}, bf16[128,128]{1,0:T(8,128)(2,1)S(1)}, u32[]{:S(2)}, u32[]{:S(2)}) collective-permute-start(bf16[128,128]{1,0:T(8,128)(2,1)S(1)} %get-tuple-element.22), channel_id=1, source_target_pairs={{0,24},{1,25},{2,26},{3,27},{4,28},{5,29},{6,30},{7,31},{8,16},{9,... | collective-permute-start | bytes 98312 | tf_op jit(solution)/shard_map/ppermute | solution.py:391
  39.2 0.0 copy-done.5
  39.2 0.3 shard_map.110.refs_1_
  39.6 0.0 collective-permute-done.3
  39.6 1.7 %collective-permute-done.2 = bf16[128,128]{1,0:T(8,128)(2,1)S(1)} collective-permute-done((bf16[128,128]{1,0:T(8,128)(2,1)S(1)}, bf16[128,128]{1,0:T(8,128)(2,1)S(1)}, u32[]{:S(2)}, u32[]{:S(2)}) %collective-permute-start.2) | collective-permute-done | bytes 32800 | tf_op jit(solution)/shard_map/ppermute | solution.py:391
  41.3 1.2 %collective-permute-done.1 = bf16[128,128]{1,0:T(8,128)(2,1)S(1)} collective-permute-done((bf16[128,128]{1,0:T(8,128)(2,1)S(1)}, bf16[128,128]{1,0:T(8,128)(2,1)S(1)}, u32[]{:S(2)}, u32[]{:S(2)}) %collective-permute-start.1) | collective-permute-done | bytes 32800 | tf_op jit(solution)/shard_map/ppermute | solution.py:391
  42.5 0.6 %collective-permute-start.6 = (bf16[512,128]{1,0:T(8,128)(2,1)S(1)}, bf16[512,128]{1,0:T(8,128)(2,1)S(1)}, u32[]{:S(2)}, u32[]{:S(2)}) collective-permute-start(bf16[512,128]{1,0:T(8,128)(2,1)S(1)} %pad_maximum_fusion.1), channel_id=1, source_target_pairs={{0,2},{1,3},{2,0},{3,1},{4,6},{5,7},{6,4},{7,5},{8,10},{9,11},{10,... | collective-permute-start | bytes 393224 | tf_op jit(solution)/shard_map/ppermute | solution.py:391
  43.1 1.3 %collective-permute-start.5 = (bf16[512,128]{1,0:T(8,128)(2,1)S(1)}, bf16[512,128]{1,0:T(8,128)(2,1)S(1)}, u32[]{:S(2)}, u32[]{:S(2)}) collective-permute-start(bf16[512,128]{1,0:T(8,128)(2,1)S(1)} %pad_maximum_fusion.1), channel_id=1, source_target_pairs={{0,4},{1,5},{2,6},{3,7},{4,0},{5,1},{6,2},{7,3},{8,12},{9,13},{10,... | collective-permute-start | bytes 393224 | tf_op jit(solution)/shard_map/ppermute | solution.py:391
  44.4 1.7 %collective-permute-start.4 = (bf16[512,128]{1,0:T(8,128)(2,1)S(1)}, bf16[512,128]{1,0:T(8,128)(2,1)S(1)}, u32[]{:S(2)}, u32[]{:S(2)}) collective-permute-start(bf16[512,128]{1,0:T(8,128)(2,1)S(1)} %pad_maximum_fusion.1), channel_id=1, source_target_pairs={{0,6},{1,7},{2,4},{3,5},{4,2},{5,3},{6,0},{7,1},{8,14},{9,15},{10,... | collective-permute-start | bytes 393224 | tf_op jit(solution)/shard_map/ppermute | solution.py:391
  46.0 0.9 %shard_map.109 = bf16[1024,128]{1,0:T(8,128)(2,1)} custom-call(f32[512,256]{1,0:T(8,128)S(1)} %get-tuple-element.20.lines_ref), custom_call_target="tpu_custom_call" | custom-call | flops 1000000000 | tf_op jit(solution)/shard_map/pallas_call | solution.py:37
  46.9 1.0 %collective-permute-done.6 = bf16[512,128]{1,0:T(8,128)(2,1)S(1)} collective-permute-done((bf16[512,128]{1,0:T(8,128)(2,1)S(1)}, bf16[512,128]{1,0:T(8,128)(2,1)S(1)}, u32[]{:S(2)}, u32[]{:S(2)}) %collective-permute-start.6) | collective-permute-done | bytes 131104 | tf_op jit(solution)/shard_map/ppermute | solution.py:391
  47.9 0.5 collective-permute-done.5
  48.4 1.8 %collective-permute-done.4 = bf16[512,128]{1,0:T(8,128)(2,1)S(1)} collective-permute-done((bf16[512,128]{1,0:T(8,128)(2,1)S(1)}, bf16[512,128]{1,0:T(8,128)(2,1)S(1)}, u32[]{:S(2)}, u32[]{:S(2)}) %collective-permute-start.4) | collective-permute-done | bytes 131104 | tf_op jit(solution)/shard_map/ppermute | solution.py:391
  50.3 0.0 copy-start.1
  50.3 0.1 collective-permute-start.7
  50.4 0.5 shard_map.111.refs_2_
  50.9 1.4 %collective-permute-done.7.refs_0_ = bf16[2048,128]{1,0:T(8,128)(2,1)S(1)} collective-permute-done((bf16[2048,128]{1,0:T(8,128)(2,1)S(1)}, bf16[2048,128]{1,0:T(8,128)(2,1)S(1)}, u32[]{:S(2)}, u32[]{:S(2)}) %collective-permute-start.7) | collective-permute-done | bytes 524320 | tf_op jit(solution)/shard_map/ppermute | solution.py:391
  52.3 0.0 copy-done.1
  52.3 1.7 %shard_map.112 = bf16[4,128,128]{2,1,0:T(8,128)(2,1)} custom-call(s32[1]{0:T(128)} %bitcast.me_ref, bf16[128,128]{1,0:T(8,128)(2,1)S(1)} %get-tuple-element.21.left_ref, bf16[2048,128]{1,0:T(8,128)(2,1)S(1)} %collective-permute-done.7.refs_0_, bf16[2048,256]{1,0:T(8,128)(2,1)S(1)} %shard_map.110.refs_1_, bf16[128,2048]{1,0:T(8,128)(2,1)S(1)} %shard_map.111.refs_2_, ...), custom_call_target="tpu_custom_call" | custom-call | tf_op jit(solution)/shard_map/pallas_call | solution.py:37
  (2 shorter events, 0.0 us)
Async XLA Ops:
  0.6 17.9 %copy-start.2 = (bf16[256,256]{1,0:T(8,128)(2,1)S(1)}, bf16[256,256]{1,0:T(8,128)(2,1)}, u32[]{:S(2)}) copy-start(bf16[256,256]{1,0:T(8,128)(2,1)} %exit_ref.4) | copy-start | bytes 393220
  2.8 15.5 %all-to-all-start = ((bf16[32,16,128]{2,1,0:T(8,128)(2,1)}), bf16[32,16,128]{2,1,0:T(8,128)(2,1)S(1)}, u32[]{:S(2)}, u32[]{:S(2)}) async-start(bf16[32,16,128]{2,1,0:T(8,128)(2,1)} %bitcast.2), calls=%async_computation | async-start | bytes 262144 | tf_op jit(solution)/shard_map/all_to_all | solution.py:427
  18.4 1.3 %collective-permute-start = (bf16[512,128]{1,0:T(8,128)(2,1)S(1)}, bf16[512,128]{1,0:T(8,128)(2,1)S(1)}, u32[]{:S(2)}, u32[]{:S(2)}) collective-permute-start(bf16[512,128]{1,0:T(8,128)(2,1)S(1)} %bitcast.14), channel_id=1, source_target_pairs={{0,1},{1,0},{2,3},{3,2},{4,5},{5,4},{6,7},{7,6},{8,9},{9,8},{10,11... | collective-permute-start | bytes 393224 | tf_op jit(solution)/shard_map/ppermute | solution.py:439
  19.2 13.5 %copy-start = (bf16[256,1024]{1,0:T(8,128)(2,1)S(1)}, bf16[256,1024]{1,0:T(8,128)(2,1)}, u32[]{:S(2)}) copy-start(bf16[256,1024]{1,0:T(8,128)(2,1)} %maps_ref.3) | copy-start | bytes 1572868
  19.2 13.5 %copy-start.3 = (bf16[256,256]{1,0:T(8,128)(2,1)S(1)}, bf16[256,256]{1,0:T(8,128)(2,1)}, u32[]{:S(2)}) copy-start(bf16[256,256]{1,0:T(8,128)(2,1)} %exit_ref.5) | copy-start | bytes 393220
  19.2 13.5 %copy-start.4 = (bf16[256,64]{0,1:T(8,128)(2,1)S(1)}, bf16[256,64]{0,1:T(8,128)(2,1)}, u32[]{:S(2)}) copy-start(bf16[256,64]{0,1:T(8,128)(2,1)} %param.16) | copy-start | bytes 98308
  19.3 20.0 %copy-start.5 = (bf16[1024,128]{1,0:T(8,128)(2,1)S(1)}, bf16[1024,128]{1,0:T(8,128)(2,1)}, u32[]{:S(2)}) copy-start(bf16[1024,128]{1,0:T(8,128)(2,1)} %exit_ref.6) | copy-start | bytes 786436
  34.8 4.8 %collective-permute-start.3 = (bf16[128,128]{1,0:T(8,128)(2,1)S(1)}, bf16[128,128]{1,0:T(8,128)(2,1)S(1)}, u32[]{:S(2)}, u32[]{:S(2)}) collective-permute-start(bf16[128,128]{1,0:T(8,128)(2,1)S(1)} %get-tuple-element.22), channel_id=1, source_target_pairs={{0,8},{1,9},{2,10},{3,11},{4,12},{5,13},{6,14},{7,15},{8,0},{9,1},... | collective-permute-start | bytes 98312 | tf_op jit(solution)/shard_map/ppermute | solution.py:391
  35.8 5.5 %collective-permute-start.2 = (bf16[128,128]{1,0:T(8,128)(2,1)S(1)}, bf16[128,128]{1,0:T(8,128)(2,1)S(1)}, u32[]{:S(2)}, u32[]{:S(2)}) collective-permute-start(bf16[128,128]{1,0:T(8,128)(2,1)S(1)} %get-tuple-element.22), channel_id=1, source_target_pairs={{0,16},{1,17},{2,18},{3,19},{4,20},{5,21},{6,22},{7,23},{8,24},{9,... | collective-permute-start | bytes 98312 | tf_op jit(solution)/shard_map/ppermute | solution.py:391
  36.7 5.7 %collective-permute-start.1 = (bf16[128,128]{1,0:T(8,128)(2,1)S(1)}, bf16[128,128]{1,0:T(8,128)(2,1)S(1)}, u32[]{:S(2)}, u32[]{:S(2)}) collective-permute-start(bf16[128,128]{1,0:T(8,128)(2,1)S(1)} %get-tuple-element.22), channel_id=1, source_target_pairs={{0,24},{1,25},{2,26},{3,27},{4,28},{5,29},{6,30},{7,31},{8,16},{9,... | collective-permute-start | bytes 98312 | tf_op jit(solution)/shard_map/ppermute | solution.py:391
  42.5 5.5 %collective-permute-start.6 = (bf16[512,128]{1,0:T(8,128)(2,1)S(1)}, bf16[512,128]{1,0:T(8,128)(2,1)S(1)}, u32[]{:S(2)}, u32[]{:S(2)}) collective-permute-start(bf16[512,128]{1,0:T(8,128)(2,1)S(1)} %pad_maximum_fusion.1), channel_id=1, source_target_pairs={{0,2},{1,3},{2,0},{3,1},{4,6},{5,7},{6,4},{7,5},{8,10},{9,11},{10,... | collective-permute-start | bytes 393224 | tf_op jit(solution)/shard_map/ppermute | solution.py:391
  43.1 5.3 %collective-permute-start.5 = (bf16[512,128]{1,0:T(8,128)(2,1)S(1)}, bf16[512,128]{1,0:T(8,128)(2,1)S(1)}, u32[]{:S(2)}, u32[]{:S(2)}) collective-permute-start(bf16[512,128]{1,0:T(8,128)(2,1)S(1)} %pad_maximum_fusion.1), channel_id=1, source_target_pairs={{0,4},{1,5},{2,6},{3,7},{4,0},{5,1},{6,2},{7,3},{8,12},{9,13},{10,... | collective-permute-start | bytes 393224 | tf_op jit(solution)/shard_map/ppermute | solution.py:391
  44.4 5.9 %collective-permute-start.4 = (bf16[512,128]{1,0:T(8,128)(2,1)S(1)}, bf16[512,128]{1,0:T(8,128)(2,1)S(1)}, u32[]{:S(2)}, u32[]{:S(2)}) collective-permute-start(bf16[512,128]{1,0:T(8,128)(2,1)S(1)} %pad_maximum_fusion.1), channel_id=1, source_target_pairs={{0,6},{1,7},{2,4},{3,5},{4,2},{5,3},{6,0},{7,1},{8,14},{9,15},{10,... | collective-permute-start | bytes 393224 | tf_op jit(solution)/shard_map/ppermute | solution.py:391
  50.3 2.0 %copy-start.1 = (bf16[4,128,128]{2,1,0:T(8,128)(2,1)S(1)}, bf16[4,128,128]{2,1,0:T(8,128)(2,1)}, u32[]{:S(2)}) copy-start(bf16[4,128,128]{2,1,0:T(8,128)(2,1)} %refs_3_.1) | copy-start | bytes 393220
  50.3 2.0 %collective-permute-start.7 = (bf16[2048,128]{1,0:T(8,128)(2,1)S(1)}, bf16[2048,128]{1,0:T(8,128)(2,1)S(1)}, u32[]{:S(2)}, u32[]{:S(2)}) collective-permute-start(bf16[2048,128]{1,0:T(8,128)(2,1)S(1)} %pad_maximum_fusion.right_ref), channel_id=1, source_target_pairs={{0,1},{1,0},{2,3},{3,2},{4,5},{5,4},{6,7},{7,6},{8,9},{9,8},{10,11... | collective-permute-start | bytes 1572872 | tf_op jit(solution)/shard_map/ppermute | solution.py:391
